TPU v7x, 32 devices: a whole 2x2x4 slice. The times are simulated.
32 devices in a mesh: dp: 4 (over x, y), cp: 8 (over z, core).
Axes of the slice: x: 2, y: 2, z: 4, core: 2. Of those that a mesh axis runs over, the one named last changes fastest.
Arguments:
- images: bfloat16 [128, 256, 768], P('dp', 'cp'), parts along dimension 0
- ln1_scale: float32 [768], replicated
- ln1_bias: float32 [768], replicated
- w_qkv: bfloat16 [768, 3, 12, 64], replicated
- b_qkv: float32 [3, 12, 64], replicated
- w_out: bfloat16 [12, 64, 768], replicated
- b_out: float32 [768], replicated
- ln2_scale: float32 [768], replicated
- ln2_bias: float32 [768], replicated
- w_up: bfloat16 [768, 3072], replicated
- b_up: float32 [3072], replicated
- w_down: bfloat16 [3072, 768], replicated
- b_down: float32 [768], replicated
- lnf_scale: float32 [768], replicated
- lnf_bias: float32 [768], replicated
- pool_probe: bfloat16 [1, 768], replicated
- pool_wq: bfloat16 [768, 12, 64], replicated
- pool_bq: float32 [12, 64], replicated
- pool_wkv: bfloat16 [768, 2, 12, 64], replicated
- pool_bkv: float32 [2, 12, 64], replicated
- pool_wout: bfloat16 [12, 64, 768], replicated
- pool_bout: float32 [768], replicated
- pool_ln_scale: float32 [768], replicated
- pool_ln_bias: float32 [768], replicated
- pool_w_up: bfloat16 [768, 3072], replicated
- pool_b_up: float32 [3072], replicated
- pool_w_down: bfloat16 [3072, 768], replicated
- pool_b_down: float32 [768], replicated
Outputs:
- output: float32 [128, 768], P('dp'), parts along dimension 0
There are 4 independent parts. A program takes and returns all parts, laid end to end along the dimension named above; an argument that names none is the same for every part.
All inputs are finite; a program needn't handle non-finite values.
Results may differ from a plain program's by a relative error of at most 0.00999552.
Values are sent between devices in bfloat16 or wider.
A program may use at most 1 GiB of HBM per device.

v0:
```python
import jax
import jax.numpy as jnp
from jax import lax
from jax.sharding import PartitionSpec as P

EPSILON = 1e-6


def layer_norm(values, ln_gain, ln_shift):
    row_mean = jnp.mean(values, axis=-1, keepdims=True)
    centered = values - row_mean
    variance = jnp.mean(centered * centered, axis=-1, keepdims=True)
    return centered * lax.rsqrt(variance + EPSILON) * ln_gain + ln_shift


def project(normed, weight, bias_vec):
    return (jnp.einsum("bnd,dhe->bnhe", normed, weight, preferred_element_type=jnp.float32) + bias_vec).astype(jnp.bfloat16)


def block_stats(queries, key_rows, value_rows, score_scale):
    scores = jnp.einsum("bqhe,bkhe->bhqk", queries, key_rows, preferred_element_type=jnp.float32) * score_scale
    row_max = jnp.max(scores, axis=-1)
    weights = jnp.exp(scores - row_max[..., None])
    value_sum = jnp.einsum("bhqk,bkhe->bhqe", weights.astype(jnp.bfloat16), value_rows, preferred_element_type=jnp.float32)
    return row_max, jnp.sum(weights, axis=-1), value_sum


def merge_stats(first_stats, second_stats):
    first_max, first_sum, first_val = first_stats
    second_max, second_sum, second_val = second_stats
    joint_max = jnp.maximum(first_max, second_max)
    first_factor = jnp.exp(first_max - joint_max)
    second_factor = jnp.exp(second_max - joint_max)
    joint_sum = first_sum * first_factor + second_sum * second_factor
    joint_val = first_val * first_factor[..., None] + second_val * second_factor[..., None]
    return joint_max, joint_sum, joint_val


def token_tail(resid_in, context, w_out, b_out, ln2_scale, ln2_bias, w_up, b_up, w_down, b_down, lnf_scale, lnf_bias):
    attn_out = jnp.einsum("cirf,ife->cre", context, w_out, preferred_element_type=jnp.float32) + b_out
    resid_mid = (resid_in + attn_out).astype(jnp.bfloat16)
    normed_mid = layer_norm(resid_mid.astype(jnp.float32), ln2_scale, ln2_bias).astype(jnp.bfloat16)
    hidden = jax.nn.gelu(jnp.einsum("bnd,df->bnf", normed_mid, w_up, preferred_element_type=jnp.float32) + b_up, approximate=True).astype(jnp.bfloat16)
    layer_out = (resid_mid.astype(jnp.float32) + jnp.einsum("bnf,fd->bnd", hidden, w_down, preferred_element_type=jnp.float32) + b_down).astype(jnp.bfloat16)
    return layer_norm(layer_out.astype(jnp.float32), lnf_scale, lnf_bias).astype(jnp.bfloat16)


def pool_stats(tokens_out, pool_probe, pool_wq, pool_bq, pool_wkv, pool_bkv, score_scale):
    probe_q = (jnp.einsum("od,dhe->he", pool_probe, pool_wq, preferred_element_type=jnp.float32) + pool_bq).astype(jnp.bfloat16)
    pool_keys = project(tokens_out, pool_wkv[:, 0], pool_bkv[0])
    pool_vals = project(tokens_out, pool_wkv[:, 1], pool_bkv[1])
    pool_scores = jnp.einsum("he,bnhe->bhn", probe_q, pool_keys, preferred_element_type=jnp.float32) * score_scale
    local_max = jnp.max(pool_scores, axis=-1)
    pool_weights = jnp.exp(pool_scores - local_max[..., None])
    local_val = jnp.einsum("bhn,bnhe->bhe", pool_weights.astype(jnp.bfloat16), pool_vals, preferred_element_type=jnp.float32)
    return jnp.concatenate([local_max[..., None], jnp.sum(pool_weights, axis=-1)[..., None], local_val], axis=-1)


def pool_finish(gathered, pool_wout, pool_bout, pool_ln_scale, pool_ln_bias, pool_w_up, pool_b_up, pool_w_down, pool_b_down):
    group_max = jnp.max(gathered[..., 0], axis=0)
    factors = jnp.exp(gathered[..., 0] - group_max)
    total_sum = jnp.sum(factors * gathered[..., 1], axis=0)
    total_val = jnp.sum(factors[..., None] * gathered[..., 2:], axis=0)
    pooled = (total_val / total_sum[..., None]).astype(jnp.bfloat16)
    pooled_out = (jnp.einsum("bhe,hed->bd", pooled, pool_wout, preferred_element_type=jnp.float32) + pool_bout).astype(jnp.bfloat16)
    normed_out = layer_norm(pooled_out.astype(jnp.float32), pool_ln_scale, pool_ln_bias).astype(jnp.bfloat16)
    hidden_out = jax.nn.gelu(jnp.dot(normed_out, pool_w_up, preferred_element_type=jnp.float32) + pool_b_up, approximate=True).astype(jnp.bfloat16)
    return pooled_out.astype(jnp.float32) + jnp.dot(hidden_out, pool_w_down, preferred_element_type=jnp.float32) + pool_b_down


def solution(mesh):
    group_size = mesh.shape["cp"]
    send_pairs = [(source, (source + 1) % group_size) for source in range(group_size)]

    def device_step(images, ln1_scale, ln1_bias, w_qkv, b_qkv, w_out, b_out, ln2_scale, ln2_bias, w_up, b_up, w_down, b_down, lnf_scale, lnf_bias, pool_probe, pool_wq, pool_bq, pool_wkv, pool_bkv, pool_wout, pool_bout, pool_ln_scale, pool_ln_bias, pool_w_up, pool_b_up, pool_w_down, pool_b_down):
        score_scale = w_qkv.shape[-1] ** -0.5
        resid_in = images.astype(jnp.float32)
        normed = layer_norm(resid_in, ln1_scale, ln1_bias).astype(jnp.bfloat16)
        queries = project(normed, w_qkv[:, 0], b_qkv[0])
        key_rows = project(normed, w_qkv[:, 1], b_qkv[1])
        value_rows = project(normed, w_qkv[:, 2], b_qkv[2])
        attn_stats = block_stats(queries, key_rows, value_rows, score_scale)

        def visit_block(step_idx, loop_state):
            held_kv, running = loop_state
            held_kv = lax.ppermute(held_kv, "cp", send_pairs)
            running = merge_stats(running, block_stats(queries, held_kv[0], held_kv[1], score_scale))
            return held_kv, running

        attn_stats = lax.fori_loop(0, group_size - 1, visit_block, ((key_rows, value_rows), attn_stats))[1]
        context = (attn_stats[2] / attn_stats[1][..., None]).astype(jnp.bfloat16)
        tokens_out = token_tail(resid_in, context, w_out, b_out, ln2_scale, ln2_bias, w_up, b_up, w_down, b_down, lnf_scale, lnf_bias)
        local_stats = pool_stats(tokens_out, pool_probe, pool_wq, pool_bq, pool_wkv, pool_bkv, score_scale)
        gathered = lax.all_gather(local_stats, "cp")
        return pool_finish(gathered, pool_wout, pool_bout, pool_ln_scale, pool_ln_bias, pool_w_up, pool_b_up, pool_w_down, pool_b_down)

    in_specs = (P("dp", "cp", None),) + (P(),) * 27
    return jax.shard_map(device_step, mesh=mesh, in_specs=in_specs, out_specs=P("dp", None), check_vma=False)
```

profile of v0, /device:TPU:0, one launch (start us, length us, event | category | flops | bytes accessed | tf_op | source)
XLA Modules:
  0.0 706.9 jit_solution(11885988998050430844)
XLA Ops:
  3.9 4.5 add_convert_fusion.2
  22.6 620.8 %while.18 = (s32[]{:T(128)}, bf16[32,32,12,64]{3,1,2,0:T(8,128)(2,1)}, bf16[32,32,12,64]{3,1,2,0:T(8,128)(2,1)}, f32[32,12,32]{2,1,0:T(8,128)S(1)}, f32[32,12,32...) while((s32[]{:T(128)}, ...), condition=%wide.region_7.0_spmd, body=%wide.region_4.0_spmd.sunk | while | flops 106217472 | bytes 73040144 | solution.py:90
  26.1 36.3 %collective-permute-done = bf16[32,32,12,64]{3,1,2,0:T(8,128)(2,1)} collective-permute-done((bf16[32,32,12,64]{3,1,2,0:T(8,128)(2,1)}, bf16[32,32,12,64]{3,1,2,0:T(8,128)(2,1)}, u32[]{:S(2)}, u32[]{:S(2)}) %collective-permute-start) | collective-permute-done | bytes 1572896 | tf_op jit(solution)/shard_map/while/body/eval_jaxpr/ppermute | solution.py:86
  62.4 4.4 copy.93
  72.9 23.2 %collective-permute-done.1 = bf16[32,32,12,64]{3,1,2,0:T(8,128)(2,1)} collective-permute-done((bf16[32,32,12,64]{3,1,2,0:T(8,128)(2,1)}, bf16[32,32,12,64]{3,1,2,0:T(8,128)(2,1)}, u32[]{:S(2)}, u32[]{:S(2)}) %collective-permute-start.1) | collective-permute-done | bytes 1572896 | tf_op jit(solution)/shard_map/while/body/eval_jaxpr/ppermute | solution.py:86
  100.5 9.2 %multiply_add_fusion.5 = f32[32,12,32,64]{3,2,1,0:T(8,128)S(1)} fusion(f32[32,12,32,64]{3,2,1,0:T(8,128)S(1)} %bitcast.122, f32[32,12,32]{2,1,0:T(8,128)S(1)} %get-tuple-element.138, f32[32,12,32]{2,1,0:T(8,128)S(1)} %get-tuple-element.139, bf16[32,32,12,64]{3,1,2,0:T(8,128)(2,1)} %collective-permute-done.1, ...), kind=kOutput, calls=%fused_computation.clone.1 | convolution fusion | flops 53870592 | bytes 9584640 | tf_op jit(solution)/shard_map/while/body/eval_jaxpr/bhqk,bkhe->bhqe/dot_general | solution.py:24
  112.8 38.1 %collective-permute-done = bf16[32,32,12,64]{3,1,2,0:T(8,128)(2,1)} collective-permute-done((bf16[32,32,12,64]{3,1,2,0:T(8,128)(2,1)}, bf16[32,32,12,64]{3,1,2,0:T(8,128)(2,1)}, u32[]{:S(2)}, u32[]{:S(2)}) %collective-permute-start) | collective-permute-done | bytes 1572896 | tf_op jit(solution)/shard_map/while/body/eval_jaxpr/ppermute | solution.py:86
  150.9 4.4 copy.93
  161.4 23.2 %collective-permute-done.1 = bf16[32,32,12,64]{3,1,2,0:T(8,128)(2,1)} collective-permute-done((bf16[32,32,12,64]{3,1,2,0:T(8,128)(2,1)}, bf16[32,32,12,64]{3,1,2,0:T(8,128)(2,1)}, u32[]{:S(2)}, u32[]{:S(2)}) %collective-permute-start.1) | collective-permute-done | bytes 1572896 | tf_op jit(solution)/shard_map/while/body/eval_jaxpr/ppermute | solution.py:86
  189.0 9.2 %multiply_add_fusion.5 = f32[32,12,32,64]{3,2,1,0:T(8,128)S(1)} fusion(f32[32,12,32,64]{3,2,1,0:T(8,128)S(1)} %bitcast.122, f32[32,12,32]{2,1,0:T(8,128)S(1)} %get-tuple-element.138, f32[32,12,32]{2,1,0:T(8,128)S(1)} %get-tuple-element.139, bf16[32,32,12,64]{3,1,2,0:T(8,128)(2,1)} %collective-permute-done.1, ...), kind=kOutput, calls=%fused_computation.clone.1 | convolution fusion | flops 53870592 | bytes 9584640 | tf_op jit(solution)/shard_map/while/body/eval_jaxpr/bhqk,bkhe->bhqe/dot_general | solution.py:24
  200.9 38.5 %collective-permute-done = bf16[32,32,12,64]{3,1,2,0:T(8,128)(2,1)} collective-permute-done((bf16[32,32,12,64]{3,1,2,0:T(8,128)(2,1)}, bf16[32,32,12,64]{3,1,2,0:T(8,128)(2,1)}, u32[]{:S(2)}, u32[]{:S(2)}) %collective-permute-start) | collective-permute-done | bytes 1572896 | tf_op jit(solution)/shard_map/while/body/eval_jaxpr/ppermute | solution.py:86
  249.9 23.2 %collective-permute-done.1 = bf16[32,32,12,64]{3,1,2,0:T(8,128)(2,1)} collective-permute-done((bf16[32,32,12,64]{3,1,2,0:T(8,128)(2,1)}, bf16[32,32,12,64]{3,1,2,0:T(8,128)(2,1)}, u32[]{:S(2)}, u32[]{:S(2)}) %collective-permute-start.1) | collective-permute-done | bytes 1572896 | tf_op jit(solution)/shard_map/while/body/eval_jaxpr/ppermute | solution.py:86
  277.5 9.2 %multiply_add_fusion.5 = f32[32,12,32,64]{3,2,1,0:T(8,128)S(1)} fusion(f32[32,12,32,64]{3,2,1,0:T(8,128)S(1)} %bitcast.122, f32[32,12,32]{2,1,0:T(8,128)S(1)} %get-tuple-element.138, f32[32,12,32]{2,1,0:T(8,128)S(1)} %get-tuple-element.139, bf16[32,32,12,64]{3,1,2,0:T(8,128)(2,1)} %collective-permute-done.1, ...), kind=kOutput, calls=%fused_computation.clone.1 | convolution fusion | flops 53870592 | bytes 9584640 | tf_op jit(solution)/shard_map/while/body/eval_jaxpr/bhqk,bkhe->bhqe/dot_general | solution.py:24
  289.4 38.5 %collective-permute-done = bf16[32,32,12,64]{3,1,2,0:T(8,128)(2,1)} collective-permute-done((bf16[32,32,12,64]{3,1,2,0:T(8,128)(2,1)}, bf16[32,32,12,64]{3,1,2,0:T(8,128)(2,1)}, u32[]{:S(2)}, u32[]{:S(2)}) %collective-permute-start) | collective-permute-done | bytes 1572896 | tf_op jit(solution)/shard_map/while/body/eval_jaxpr/ppermute | solution.py:86
  327.9 4.4 copy.93
  338.4 23.2 %collective-permute-done.1 = bf16[32,32,12,64]{3,1,2,0:T(8,128)(2,1)} collective-permute-done((bf16[32,32,12,64]{3,1,2,0:T(8,128)(2,1)}, bf16[32,32,12,64]{3,1,2,0:T(8,128)(2,1)}, u32[]{:S(2)}, u32[]{:S(2)}) %collective-permute-start.1) | collective-permute-done | bytes 1572896 | tf_op jit(solution)/shard_map/while/body/eval_jaxpr/ppermute | solution.py:86
  366.1 9.2 %multiply_add_fusion.5 = f32[32,12,32,64]{3,2,1,0:T(8,128)S(1)} fusion(f32[32,12,32,64]{3,2,1,0:T(8,128)S(1)} %bitcast.122, f32[32,12,32]{2,1,0:T(8,128)S(1)} %get-tuple-element.138, f32[32,12,32]{2,1,0:T(8,128)S(1)} %get-tuple-element.139, bf16[32,32,12,64]{3,1,2,0:T(8,128)(2,1)} %collective-permute-done.1, ...), kind=kOutput, calls=%fused_computation.clone.1 | convolution fusion | flops 53870592 | bytes 9584640 | tf_op jit(solution)/shard_map/while/body/eval_jaxpr/bhqk,bkhe->bhqe/dot_general | solution.py:24
  377.9 38.5 %collective-permute-done = bf16[32,32,12,64]{3,1,2,0:T(8,128)(2,1)} collective-permute-done((bf16[32,32,12,64]{3,1,2,0:T(8,128)(2,1)}, bf16[32,32,12,64]{3,1,2,0:T(8,128)(2,1)}, u32[]{:S(2)}, u32[]{:S(2)}) %collective-permute-start) | collective-permute-done | bytes 1572896 | tf_op jit(solution)/shard_map/while/body/eval_jaxpr/ppermute | solution.py:86
  426.9 23.2 %collective-permute-done.1 = bf16[32,32,12,64]{3,1,2,0:T(8,128)(2,1)} collective-permute-done((bf16[32,32,12,64]{3,1,2,0:T(8,128)(2,1)}, bf16[32,32,12,64]{3,1,2,0:T(8,128)(2,1)}, u32[]{:S(2)}, u32[]{:S(2)}) %collective-permute-start.1) | collective-permute-done | bytes 1572896 | tf_op jit(solution)/shard_map/while/body/eval_jaxpr/ppermute | solution.py:86
  454.6 9.2 %multiply_add_fusion.5 = f32[32,12,32,64]{3,2,1,0:T(8,128)S(1)} fusion(f32[32,12,32,64]{3,2,1,0:T(8,128)S(1)} %bitcast.122, f32[32,12,32]{2,1,0:T(8,128)S(1)} %get-tuple-element.138, f32[32,12,32]{2,1,0:T(8,128)S(1)} %get-tuple-element.139, bf16[32,32,12,64]{3,1,2,0:T(8,128)(2,1)} %collective-permute-done.1, ...), kind=kOutput, calls=%fused_computation.clone.1 | convolution fusion | flops 53870592 | bytes 9584640 | tf_op jit(solution)/shard_map/while/body/eval_jaxpr/bhqk,bkhe->bhqe/dot_general | solution.py:24
  466.4 38.5 %collective-permute-done = bf16[32,32,12,64]{3,1,2,0:T(8,128)(2,1)} collective-permute-done((bf16[32,32,12,64]{3,1,2,0:T(8,128)(2,1)}, bf16[32,32,12,64]{3,1,2,0:T(8,128)(2,1)}, u32[]{:S(2)}, u32[]{:S(2)}) %collective-permute-start) | collective-permute-done | bytes 1572896 | tf_op jit(solution)/shard_map/while/body/eval_jaxpr/ppermute | solution.py:86
  515.4 23.2 %collective-permute-done.1 = bf16[32,32,12,64]{3,1,2,0:T(8,128)(2,1)} collective-permute-done((bf16[32,32,12,64]{3,1,2,0:T(8,128)(2,1)}, bf16[32,32,12,64]{3,1,2,0:T(8,128)(2,1)}, u32[]{:S(2)}, u32[]{:S(2)}) %collective-permute-start.1) | collective-permute-done | bytes 1572896 | tf_op jit(solution)/shard_map/while/body/eval_jaxpr/ppermute | solution.py:86
  543.1 9.2 %multiply_add_fusion.5 = f32[32,12,32,64]{3,2,1,0:T(8,128)S(1)} fusion(f32[32,12,32,64]{3,2,1,0:T(8,128)S(1)} %bitcast.122, f32[32,12,32]{2,1,0:T(8,128)S(1)} %get-tuple-element.138, f32[32,12,32]{2,1,0:T(8,128)S(1)} %get-tuple-element.139, bf16[32,32,12,64]{3,1,2,0:T(8,128)(2,1)} %collective-permute-done.1, ...), kind=kOutput, calls=%fused_computation.clone.1 | convolution fusion | flops 53870592 | bytes 9584640 | tf_op jit(solution)/shard_map/while/body/eval_jaxpr/bhqk,bkhe->bhqe/dot_general | solution.py:24
  554.9 38.5 %collective-permute-done = bf16[32,32,12,64]{3,1,2,0:T(8,128)(2,1)} collective-permute-done((bf16[32,32,12,64]{3,1,2,0:T(8,128)(2,1)}, bf16[32,32,12,64]{3,1,2,0:T(8,128)(2,1)}, u32[]{:S(2)}, u32[]{:S(2)}) %collective-permute-start) | collective-permute-done | bytes 1572896 | tf_op jit(solution)/shard_map/while/body/eval_jaxpr/ppermute | solution.py:86
  603.9 23.2 %collective-permute-done.1 = bf16[32,32,12,64]{3,1,2,0:T(8,128)(2,1)} collective-permute-done((bf16[32,32,12,64]{3,1,2,0:T(8,128)(2,1)}, bf16[32,32,12,64]{3,1,2,0:T(8,128)(2,1)}, u32[]{:S(2)}, u32[]{:S(2)}) %collective-permute-start.1) | collective-permute-done | bytes 1572896 | tf_op jit(solution)/shard_map/while/body/eval_jaxpr/ppermute | solution.py:86
  631.6 9.2 %multiply_add_fusion.5 = f32[32,12,32,64]{3,2,1,0:T(8,128)S(1)} fusion(f32[32,12,32,64]{3,2,1,0:T(8,128)S(1)} %bitcast.122, f32[32,12,32]{2,1,0:T(8,128)S(1)} %get-tuple-element.138, f32[32,12,32]{2,1,0:T(8,128)S(1)} %get-tuple-element.139, bf16[32,32,12,64]{3,1,2,0:T(8,128)(2,1)} %collective-permute-done.1, ...), kind=kOutput, calls=%fused_computation.clone.1 | convolution fusion | flops 53870592 | bytes 9584640 | tf_op jit(solution)/shard_map/while/body/eval_jaxpr/bhqk,bkhe->bhqe/dot_general | solution.py:24
  643.5 5.5 convert_reduce_fusion
  649.7 5.2 fusion.22
  655.0 8.4 %convert_reduce_fusion.2 = (f32[32,32]{1,0:T(8,128)S(1)}, bf16[32,32,768]{2,1,0:T(8,128)(2,1)S(1)}) fusion(f32[768]{0:T(1024)S(1)} %copy-done.26, bf16[3072,768]{1,0:T(8,128)(2,1)S(1)} %bitcast.132, f32[32,32,3072]{2,1,0:T(8,128)S(1)} %fusion.22, f32[3072]{0:T(1024)S(1)} %copy-done.20, bf16[32,32,768]{2,1,0:T(8,128)(2,1)S(1)} %get-tuple-element.78), kind=kOutput, calls=%fused_computation.42 | convolution fusion | flops 4868013056 | bytes 20466688 | tf_op jit(solution)/shard_map/bnf,fd->bnd/dot_general | solution.py:44
  672.6 4.8 fusion.47
  677.9 18.6 %all-gather = f32[256,12,66]{2,0,1:T(8,128)S(1)} all-gather(f32[32,12,66]{2,0,1:T(8,128)S(1)} %pad_maximum_fusion), channel_id=2, replica_groups=mesh['dp'=4,'cp'=8] {'cp'}, dimensions={0}, use_global_device_ids=true | all-gather | bytes 912384 | tf_op jit(solution)/shard_map/all_gather | solution.py:94
  700.3 6.2 fusion.81
  (206 shorter events, 145.1 us)
Async XLA Ops:
  0.0 643.4 %copy-start = (bf16[12,64,768]{2,1,0:T(8,128)(2,1)S(1)}, bf16[12,64,768]{2,1,0:T(8,128)(2,1)}, u32[]{:S(2)}) copy-start(bf16[12,64,768]{2,1,0:T(8,128)(2,1)} %param.35) | copy-start | bytes 3538948
  22.6 620.8 %copy-start.23 = (f32[768]{0:T(1024)S(1)}, f32[768]{0:T(1024)}, u32[]{:S(2)}) copy-start(f32[768]{0:T(1024)} %param.36) | copy-start | bytes 9220
  22.8 39.6 %collective-permute-start = (bf16[32,32,12,64]{3,1,2,0:T(8,128)(2,1)}, bf16[32,32,12,64]{3,1,2,0:T(8,128)(2,1)}, u32[]{:S(2)}, u32[]{:S(2)}) collective-permute-start(bf16[32,32,12,64]{3,1,2,0:T(8,128)(2,1)} %get-tuple-element.149), channel_id=1, source_target_pairs={{0,1},{1,2},{2,3},{3,4},{4,5},{5,6},{6,7},{7,0},{8,9},{9,10},{10,1... | collective-permute-start | bytes 4718600 | tf_op jit(solution)/shard_map/while/body/eval_jaxpr/ppermute | solution.py:86
  23.4 72.7 %collective-permute-start.1 = (bf16[32,32,12,64]{3,1,2,0:T(8,128)(2,1)}, bf16[32,32,12,64]{3,1,2,0:T(8,128)(2,1)}, u32[]{:S(2)}, u32[]{:S(2)}) collective-permute-start(bf16[32,32,12,64]{3,1,2,0:T(8,128)(2,1)} %get-tuple-element.150), channel_id=1, source_target_pairs={{0,1},{1,2},{2,3},{3,4},{4,5},{5,6},{6,7},{7,0},{8,9},{9,10},{10,1... | collective-permute-start | bytes 4718600 | tf_op jit(solution)/shard_map/while/body/eval_jaxpr/ppermute | solution.py:86
  26.1 40.7 %copy-start.3 = (bf16[32,32,12,64]{3,1,2,0:T(8,128)(2,1)S(1)}, bf16[32,32,12,64]{3,1,2,0:T(8,128)(2,1)}, u32[]{:S(2)}) copy-start(bf16[32,32,12,64]{3,1,2,0:T(8,128)(2,1)} %get-tuple-element.162) | copy-start | bytes 4718596 | tf_op jit(solution)/shard_map/while
  70.5 30.0 %slice-start = ((s8[6291456]{0:T(1024)(128)(4,1)}), s8[4194304]{0:T(1024)(128)(4,1)S(1)}, s32[]{:S(2)}) async-start(s8[6291456]{0:T(1024)(128)(4,1)} %bitcast.121), calls=%async_computation | async-start | bytes 8388608 | tf_op jit(solution)/shard_map/while
  112.4 38.5 %collective-permute-start = (bf16[32,32,12,64]{3,1,2,0:T(8,128)(2,1)}, bf16[32,32,12,64]{3,1,2,0:T(8,128)(2,1)}, u32[]{:S(2)}, u32[]{:S(2)}) collective-permute-start(bf16[32,32,12,64]{3,1,2,0:T(8,128)(2,1)} %get-tuple-element.149), channel_id=1, source_target_pairs={{0,1},{1,2},{2,3},{3,4},{4,5},{5,6},{6,7},{7,0},{8,9},{9,10},{10,1... | collective-permute-start | bytes 4718600 | tf_op jit(solution)/shard_map/while/body/eval_jaxpr/ppermute | solution.py:86
  112.4 72.2 %collective-permute-start.1 = (bf16[32,32,12,64]{3,1,2,0:T(8,128)(2,1)}, bf16[32,32,12,64]{3,1,2,0:T(8,128)(2,1)}, u32[]{:S(2)}, u32[]{:S(2)}) collective-permute-start(bf16[32,32,12,64]{3,1,2,0:T(8,128)(2,1)} %get-tuple-element.150), channel_id=1, source_target_pairs={{0,1},{1,2},{2,3},{3,4},{4,5},{5,6},{6,7},{7,0},{8,9},{9,10},{10,1... | collective-permute-start | bytes 4718600 | tf_op jit(solution)/shard_map/while/body/eval_jaxpr/ppermute | solution.py:86
  112.8 42.5 %copy-start.3 = (bf16[32,32,12,64]{3,1,2,0:T(8,128)(2,1)S(1)}, bf16[32,32,12,64]{3,1,2,0:T(8,128)(2,1)}, u32[]{:S(2)}) copy-start(bf16[32,32,12,64]{3,1,2,0:T(8,128)(2,1)} %get-tuple-element.162) | copy-start | bytes 4718596 | tf_op jit(solution)/shard_map/while
  159.0 30.0 %slice-start = ((s8[6291456]{0:T(1024)(128)(4,1)}), s8[4194304]{0:T(1024)(128)(4,1)S(1)}, s32[]{:S(2)}) async-start(s8[6291456]{0:T(1024)(128)(4,1)} %bitcast.121), calls=%async_computation | async-start | bytes 8388608 | tf_op jit(solution)/shard_map/while
  200.9 38.5 %collective-permute-start = (bf16[32,32,12,64]{3,1,2,0:T(8,128)(2,1)}, bf16[32,32,12,64]{3,1,2,0:T(8,128)(2,1)}, u32[]{:S(2)}, u32[]{:S(2)}) collective-permute-start(bf16[32,32,12,64]{3,1,2,0:T(8,128)(2,1)} %get-tuple-element.149), channel_id=1, source_target_pairs={{0,1},{1,2},{2,3},{3,4},{4,5},{5,6},{6,7},{7,0},{8,9},{9,10},{10,1... | collective-permute-start | bytes 4718600 | tf_op jit(solution)/shard_map/while/body/eval_jaxpr/ppermute | solution.py:86
  200.9 72.2 %collective-permute-start.1 = (bf16[32,32,12,64]{3,1,2,0:T(8,128)(2,1)}, bf16[32,32,12,64]{3,1,2,0:T(8,128)(2,1)}, u32[]{:S(2)}, u32[]{:S(2)}) collective-permute-start(bf16[32,32,12,64]{3,1,2,0:T(8,128)(2,1)} %get-tuple-element.150), channel_id=1, source_target_pairs={{0,1},{1,2},{2,3},{3,4},{4,5},{5,6},{6,7},{7,0},{8,9},{9,10},{10,1... | collective-permute-start | bytes 4718600 | tf_op jit(solution)/shard_map/while/body/eval_jaxpr/ppermute | solution.py:86
  200.9 42.9 %copy-start.3 = (bf16[32,32,12,64]{3,1,2,0:T(8,128)(2,1)S(1)}, bf16[32,32,12,64]{3,1,2,0:T(8,128)(2,1)}, u32[]{:S(2)}) copy-start(bf16[32,32,12,64]{3,1,2,0:T(8,128)(2,1)} %get-tuple-element.162) | copy-start | bytes 4718596 | tf_op jit(solution)/shard_map/while
  247.5 30.0 %slice-start = ((s8[6291456]{0:T(1024)(128)(4,1)}), s8[4194304]{0:T(1024)(128)(4,1)S(1)}, s32[]{:S(2)}) async-start(s8[6291456]{0:T(1024)(128)(4,1)} %bitcast.121), calls=%async_computation | async-start | bytes 8388608 | tf_op jit(solution)/shard_map/while
  249.6 27.9 %slice-start.1 = ((s8[6291456]{0:T(1024)(128)(4,1)}), s8[2097152]{0:T(1024)(128)(4,1)S(1)}, s32[]{:S(2)}) async-start(s8[6291456]{0:T(1024)(128)(4,1)} %bitcast.121), calls=%async_computation.1 | async-start | bytes 4194304 | tf_op jit(solution)/shard_map/while
  289.4 38.5 %collective-permute-start = (bf16[32,32,12,64]{3,1,2,0:T(8,128)(2,1)}, bf16[32,32,12,64]{3,1,2,0:T(8,128)(2,1)}, u32[]{:S(2)}, u32[]{:S(2)}) collective-permute-start(bf16[32,32,12,64]{3,1,2,0:T(8,128)(2,1)} %get-tuple-element.149), channel_id=1, source_target_pairs={{0,1},{1,2},{2,3},{3,4},{4,5},{5,6},{6,7},{7,0},{8,9},{9,10},{10,1... | collective-permute-start | bytes 4718600 | tf_op jit(solution)/shard_map/while/body/eval_jaxpr/ppermute | solution.py:86
  289.4 72.2 %collective-permute-start.1 = (bf16[32,32,12,64]{3,1,2,0:T(8,128)(2,1)}, bf16[32,32,12,64]{3,1,2,0:T(8,128)(2,1)}, u32[]{:S(2)}, u32[]{:S(2)}) collective-permute-start(bf16[32,32,12,64]{3,1,2,0:T(8,128)(2,1)} %get-tuple-element.150), channel_id=1, source_target_pairs={{0,1},{1,2},{2,3},{3,4},{4,5},{5,6},{6,7},{7,0},{8,9},{9,10},{10,1... | collective-permute-start | bytes 4718600 | tf_op jit(solution)/shard_map/while/body/eval_jaxpr/ppermute | solution.py:86
  289.4 42.9 %copy-start.3 = (bf16[32,32,12,64]{3,1,2,0:T(8,128)(2,1)S(1)}, bf16[32,32,12,64]{3,1,2,0:T(8,128)(2,1)}, u32[]{:S(2)}) copy-start(bf16[32,32,12,64]{3,1,2,0:T(8,128)(2,1)} %get-tuple-element.162) | copy-start | bytes 4718596 | tf_op jit(solution)/shard_map/while
  336.0 30.0 %slice-start = ((s8[6291456]{0:T(1024)(128)(4,1)}), s8[4194304]{0:T(1024)(128)(4,1)S(1)}, s32[]{:S(2)}) async-start(s8[6291456]{0:T(1024)(128)(4,1)} %bitcast.121), calls=%async_computation | async-start | bytes 8388608 | tf_op jit(solution)/shard_map/while
  377.9 38.5 %collective-permute-start = (bf16[32,32,12,64]{3,1,2,0:T(8,128)(2,1)}, bf16[32,32,12,64]{3,1,2,0:T(8,128)(2,1)}, u32[]{:S(2)}, u32[]{:S(2)}) collective-permute-start(bf16[32,32,12,64]{3,1,2,0:T(8,128)(2,1)} %get-tuple-element.149), channel_id=1, source_target_pairs={{0,1},{1,2},{2,3},{3,4},{4,5},{5,6},{6,7},{7,0},{8,9},{9,10},{10,1... | collective-permute-start | bytes 4718600 | tf_op jit(solution)/shard_map/while/body/eval_jaxpr/ppermute | solution.py:86
  377.9 72.2 %collective-permute-start.1 = (bf16[32,32,12,64]{3,1,2,0:T(8,128)(2,1)}, bf16[32,32,12,64]{3,1,2,0:T(8,128)(2,1)}, u32[]{:S(2)}, u32[]{:S(2)}) collective-permute-start(bf16[32,32,12,64]{3,1,2,0:T(8,128)(2,1)} %get-tuple-element.150), channel_id=1, source_target_pairs={{0,1},{1,2},{2,3},{3,4},{4,5},{5,6},{6,7},{7,0},{8,9},{9,10},{10,1... | collective-permute-start | bytes 4718600 | tf_op jit(solution)/shard_map/while/body/eval_jaxpr/ppermute | solution.py:86
  377.9 42.9 %copy-start.3 = (bf16[32,32,12,64]{3,1,2,0:T(8,128)(2,1)S(1)}, bf16[32,32,12,64]{3,1,2,0:T(8,128)(2,1)}, u32[]{:S(2)}) copy-start(bf16[32,32,12,64]{3,1,2,0:T(8,128)(2,1)} %get-tuple-element.162) | copy-start | bytes 4718596 | tf_op jit(solution)/shard_map/while
  424.5 30.0 %slice-start = ((s8[6291456]{0:T(1024)(128)(4,1)}), s8[4194304]{0:T(1024)(128)(4,1)S(1)}, s32[]{:S(2)}) async-start(s8[6291456]{0:T(1024)(128)(4,1)} %bitcast.121), calls=%async_computation | async-start | bytes 8388608 | tf_op jit(solution)/shard_map/while
  426.6 27.9 %slice-start.1 = ((s8[6291456]{0:T(1024)(128)(4,1)}), s8[2097152]{0:T(1024)(128)(4,1)S(1)}, s32[]{:S(2)}) async-start(s8[6291456]{0:T(1024)(128)(4,1)} %bitcast.121), calls=%async_computation.1 | async-start | bytes 4194304 | tf_op jit(solution)/shard_map/while
  466.4 38.5 %collective-permute-start = (bf16[32,32,12,64]{3,1,2,0:T(8,128)(2,1)}, bf16[32,32,12,64]{3,1,2,0:T(8,128)(2,1)}, u32[]{:S(2)}, u32[]{:S(2)}) collective-permute-start(bf16[32,32,12,64]{3,1,2,0:T(8,128)(2,1)} %get-tuple-element.149), channel_id=1, source_target_pairs={{0,1},{1,2},{2,3},{3,4},{4,5},{5,6},{6,7},{7,0},{8,9},{9,10},{10,1... | collective-permute-start | bytes 4718600 | tf_op jit(solution)/shard_map/while/body/eval_jaxpr/ppermute | solution.py:86
  466.4 72.2 %collective-permute-start.1 = (bf16[32,32,12,64]{3,1,2,0:T(8,128)(2,1)}, bf16[32,32,12,64]{3,1,2,0:T(8,128)(2,1)}, u32[]{:S(2)}, u32[]{:S(2)}) collective-permute-start(bf16[32,32,12,64]{3,1,2,0:T(8,128)(2,1)} %get-tuple-element.150), channel_id=1, source_target_pairs={{0,1},{1,2},{2,3},{3,4},{4,5},{5,6},{6,7},{7,0},{8,9},{9,10},{10,1... | collective-permute-start | bytes 4718600 | tf_op jit(solution)/shard_map/while/body/eval_jaxpr/ppermute | solution.py:86
  466.4 42.9 %copy-start.3 = (bf16[32,32,12,64]{3,1,2,0:T(8,128)(2,1)S(1)}, bf16[32,32,12,64]{3,1,2,0:T(8,128)(2,1)}, u32[]{:S(2)}) copy-start(bf16[32,32,12,64]{3,1,2,0:T(8,128)(2,1)} %get-tuple-element.162) | copy-start | bytes 4718596 | tf_op jit(solution)/shard_map/while
  513.0 30.0 %slice-start = ((s8[6291456]{0:T(1024)(128)(4,1)}), s8[4194304]{0:T(1024)(128)(4,1)S(1)}, s32[]{:S(2)}) async-start(s8[6291456]{0:T(1024)(128)(4,1)} %bitcast.121), calls=%async_computation | async-start | bytes 8388608 | tf_op jit(solution)/shard_map/while
  554.9 38.5 %collective-permute-start = (bf16[32,32,12,64]{3,1,2,0:T(8,128)(2,1)}, bf16[32,32,12,64]{3,1,2,0:T(8,128)(2,1)}, u32[]{:S(2)}, u32[]{:S(2)}) collective-permute-start(bf16[32,32,12,64]{3,1,2,0:T(8,128)(2,1)} %get-tuple-element.149), channel_id=1, source_target_pairs={{0,1},{1,2},{2,3},{3,4},{4,5},{5,6},{6,7},{7,0},{8,9},{9,10},{10,1... | collective-permute-start | bytes 4718600 | tf_op jit(solution)/shard_map/while/body/eval_jaxpr/ppermute | solution.py:86
  554.9 72.2 %collective-permute-start.1 = (bf16[32,32,12,64]{3,1,2,0:T(8,128)(2,1)}, bf16[32,32,12,64]{3,1,2,0:T(8,128)(2,1)}, u32[]{:S(2)}, u32[]{:S(2)}) collective-permute-start(bf16[32,32,12,64]{3,1,2,0:T(8,128)(2,1)} %get-tuple-element.150), channel_id=1, source_target_pairs={{0,1},{1,2},{2,3},{3,4},{4,5},{5,6},{6,7},{7,0},{8,9},{9,10},{10,1... | collective-permute-start | bytes 4718600 | tf_op jit(solution)/shard_map/while/body/eval_jaxpr/ppermute | solution.py:86
  554.9 42.9 %copy-start.3 = (bf16[32,32,12,64]{3,1,2,0:T(8,128)(2,1)S(1)}, bf16[32,32,12,64]{3,1,2,0:T(8,128)(2,1)}, u32[]{:S(2)}) copy-start(bf16[32,32,12,64]{3,1,2,0:T(8,128)(2,1)} %get-tuple-element.162) | copy-start | bytes 4718596 | tf_op jit(solution)/shard_map/while
  601.6 30.0 %slice-start = ((s8[6291456]{0:T(1024)(128)(4,1)}), s8[4194304]{0:T(1024)(128)(4,1)S(1)}, s32[]{:S(2)}) async-start(s8[6291456]{0:T(1024)(128)(4,1)} %bitcast.121), calls=%async_computation | async-start | bytes 8388608 | tf_op jit(solution)/shard_map/while
  (40 other events, 300.4 us)
where the time goes:
time: 716 us; the launch traced here: 707 us
  waiting for transfers between devices  429 us (60%)
  matrix products  146 us (20%)
  local copies, waits for them, and re-layouts  81.3 us (11%)
  other arithmetic  26.9 us (4%)
  blocking collectives  18.6 us (3%)
    ppermute x14, waiting for transfers between devices, visit_block(): held_kv = lax.ppermute(held_kv, 'cp', send_pairs)  429 us
    while x70, local copies, waits for them, and re-layouts  80.8 us
    dot_general x8, matrix products, block_stats(): jnp.einsum('bhqk,bkhe->bhqe', weights.astype(jnp.bfloat16), value_rows, p...  68 us
    dot_general x8, matrix products, block_stats(): jnp.einsum('bqhe,bkhe->bhqk', queries, key_rows, preferred_element_type=j...  27.5 us
    all_gather x1, blocking collectives, device_step(): gathered = lax.all_gather(local_stats, 'cp')  18.6 us
    reduce_sum x8, other arithmetic, block_stats(): return (row_max, jnp.sum(weights, axis=-1), value_sum)  16.6 us
    dot_general x4, matrix products, project(): jnp.einsum('bnd,dhe->bnhe', normed, weight, preferred_element_type=jnp.fl...  14.7 us
  transfers between devices with their start and end apart: 14, of which 14 were waited for; matrix products, arithmetic and copies ran while one was open for 10% of the time, Pallas kernels for 0%

commit v1 on v0

v1 whole, which is shorter than its diff:
```python
import functools
import math

import jax
import jax.numpy as jnp
from jax import lax
from jax.experimental import pallas as pl
from jax.experimental.pallas import tpu as pltpu
from jax.sharding import PartitionSpec as P

MESH = pl.DeviceIdType.MESH
F32 = jnp.float32
BF16 = jnp.bfloat16
EPSILON = 1e-6
DIM = 768
HEADS = 12
HEAD = 64
MLP = 3072
GELU_C = math.sqrt(2.0 / math.pi)
LOG2E = math.log2(math.e)


def dot(left, right):
    return jnp.dot(left, right, preferred_element_type=F32)


def dot_nt(left, right):
    return lax.dot_general(left, right, (((1,), (1,)), ((), ())), preferred_element_type=F32)


def gelu(x):
    half = 0.5 * x
    return half + half * jnp.tanh(x * (GELU_C + (GELU_C * 0.044715) * (x * x)))


def layer_norm(values, gain, shift):
    row_mean = jnp.sum(values, axis=-1, keepdims=True) * (1.0 / DIM)
    centered = values - row_mean
    variance = jnp.sum(centered * centered, axis=-1, keepdims=True) * (1.0 / DIM)
    return centered * lax.rsqrt(variance + EPSILON) * gain + shift


def column_bias(bias, out_ref, base):
    eye = lax.broadcasted_iota(jnp.int32, (HEAD, HEAD), 0) == lax.broadcasted_iota(jnp.int32, (HEAD, HEAD), 1)
    for head in range(HEADS):
        spread = jnp.where(eye, jnp.broadcast_to(bias[head : head + 1, :], (HEAD, HEAD)), 0.0)
        column = jnp.sum(spread, axis=1, keepdims=True)
        out_ref[pl.ds(base + head * HEAD, HEAD), :] = jnp.broadcast_to(column, (HEAD, 128))


def row_bias(column_ref, base):
    eye = lax.broadcasted_iota(jnp.int32, (128, 128), 0) == lax.broadcasted_iota(jnp.int32, (128, 128), 1)
    parts = []
    for block in range(DIM // 128):
        tile = column_ref[pl.ds(base + block * 128, 128), :]
        parts.append(jnp.sum(jnp.where(eye, tile, 0.0), axis=0, keepdims=True))
    return jnp.concatenate(parts, axis=1)


def add_column(values, column):
    return values + jnp.concatenate([column, column], axis=1)


def kernel(
    group, local, run,
    images, ln1_g, ln1_c, w_qkv, b_qkv, w_out, b_out, ln2_g, ln2_c, w_up, b_up, w_down, b_down, lnf_g, lnf_c,
    probe, p_wq, p_bq, p_wkv, p_bkv, p_wout, p_bout, pln_g, pln_c, p_wup, p_bup, p_wdown, p_bdown,
    out_ref,
    x_buf, v_ln1_g, v_ln1_c, v_wqkv, v_bqkv, v_wout, v_bout, v_ln2_g, v_ln2_c, v_wup, v_bup, v_wdown, v_bdown, v_lnf_g, v_lnf_c,
    v_probe, v_pwq, v_pbq, v_pwkv, v_pbkv, v_pwout, v_pbout, v_plng, v_plnc, v_pwup, v_pbup, v_pwdown, v_pbdown,
    wk_t, col_qkv, col_q, col_kv, row_k, u_diag, h_buf, h_t, q_t, v_t, k_buf, c_t, r_buf, n_buf, m_buf, z_buf, kv_t, a_buf, emb,
    load_sem, own_sem, send_sem, recv_sem, emb_send, emb_recv,
):
    tokens = group * run
    me = lax.axis_index("cp")
    barrier = pltpu.get_barrier_semaphore()
    for k in range(1, group):
        pl.semaphore_signal(barrier, inc=1, device_id={"cp": me ^ k}, device_id_type=MESH)

    pairs = [
        (w_qkv, v_wqkv), (ln1_g, v_ln1_g), (ln1_c, v_ln1_c), (b_qkv, v_bqkv), (w_out, v_wout), (b_out, v_bout),
        (ln2_g, v_ln2_g), (ln2_c, v_ln2_c), (w_up, v_wup), (b_up, v_bup), (w_down, v_wdown), (b_down, v_bdown),
        (lnf_g, v_lnf_g), (lnf_c, v_lnf_c), (probe, v_probe), (p_wq, v_pwq), (p_bq, v_pbq), (p_wkv, v_pwkv),
        (p_bkv, v_pbkv), (p_wout, v_pwout), (p_bout, v_pbout), (pln_g, v_plng), (pln_c, v_plnc), (p_wup, v_pwup),
        (p_bup, v_pbup), (p_wdown, v_pwdown), (p_bdown, v_pbdown),
    ]
    loads = [pltpu.make_async_copy(src, dst, load_sem.at[i]) for i, (src, dst) in enumerate(pairs)]
    own = [pltpu.make_async_copy(images.at[me * local + s], x_buf.at[s, me], own_sem.at[s]) for s in range(local)]
    for copy in loads[:4]:
        copy.start()
    for copy in own:
        copy.start()

    def send(s, k):
        peer = me ^ k
        return pltpu.make_async_remote_copy(
            src_ref=images.at[peer * local + s],
            dst_ref=x_buf.at[s, me],
            send_sem=send_sem.at[s, k],
            recv_sem=recv_sem.at[s, k],
            device_id={"cp": peer},
            device_id_type=MESH,
        )

    order = sorted(range(1, group), key=lambda k: -k)
    pl.semaphore_wait(barrier, group - 1)
    for s in range(local):
        for k in order:
            send(s, k).start()
    for copy in loads[4:]:
        copy.start()
    for copy in loads[:4]:
        copy.wait()

    for part in range(3):
        column_bias(v_bqkv[part], col_qkv, part * DIM)
    row_k[...] = row_bias(col_qkv, DIM)
    for block in range(DIM // 256):
        wk_t[:, pl.ds(block * 256, 256)] = v_wqkv[pl.ds(DIM + block * 256, 256), :].T
    for copy in loads[4:]:
        copy.wait()
    column_bias(v_pbq[...], col_q, 0)
    column_bias(v_pbkv[:, 0, :], col_kv, 0)
    column_bias(v_pbkv[:, 1, :], col_kv, DIM)
    probe_rows = jnp.broadcast_to(v_probe[...].astype(F32), (16, DIM)).astype(BF16)
    probe_q = dot_nt(probe_rows, v_pwq[...]) + row_bias(col_q, 0)
    head_of_lane = lax.broadcasted_iota(jnp.int32, (16, DIM), 1) // HEAD
    diagonal = head_of_lane == lax.broadcasted_iota(jnp.int32, (16, DIM), 0)
    u_diag[...] = jnp.where(diagonal, probe_q, 0.0).astype(BF16)

    rows = 32
    a_buf[...] = jnp.zeros_like(a_buf)

    def one_image(s, _):
        pltpu.make_async_copy(images.at[0], x_buf.at[s, me], own_sem.at[s]).wait()
        for k in order:
            send(s, k).wait_recv()

        for piece in range(group):
            x = x_buf[s, piece].astype(F32)
            h_buf[pl.ds(piece * run, run), :] = layer_norm(x, v_ln1_g[...], v_ln1_c[...]).astype(BF16)
        h_t[...] = h_buf[...].T
        q_t[...] = add_column(dot(v_wqkv[pl.ds(0, DIM), :], h_t[...]), col_qkv[pl.ds(0, DIM), :]).astype(BF16)
        v_t[...] = add_column(dot(v_wqkv[pl.ds(2 * DIM, DIM), :], h_t[...]), col_qkv[pl.ds(2 * DIM, DIM), :]).astype(BF16)
        k_buf[...] = (dot(h_buf[...], wk_t[...]) + row_k[...]).astype(BF16)

        zero = jnp.zeros((HEAD, tokens), BF16)
        for pair in range(HEADS // 2):
            k_pair = k_buf[:, pl.ds(pair * 2 * HEAD, 2 * HEAD)]
            for side in range(2):
                head = 2 * pair + side
                q_head = q_t[pl.ds(head * HEAD, HEAD), :]
                q_pair = jnp.concatenate([q_head, zero] if side == 0 else [zero, q_head], axis=0)
                scores = dot(k_pair, q_pair)
                top = jnp.max(scores, axis=0, keepdims=True)
                weights = jnp.exp2((scores - top) * (LOG2E * HEAD**-0.5))
                total = jnp.sum(weights, axis=0, keepdims=True)
                value = dot(v_t[pl.ds(head * HEAD, HEAD), :], weights.astype(BF16))
                c_t[pl.ds(head * HEAD, HEAD), :] = (value / total).astype(BF16)

        h_buf[...] = c_t[...].T
        for block in range(DIM // 256):
            cols = pl.ds(block * 256, 256)
            attn = dot(h_buf[...], v_wout[:, cols]) + v_bout[:, cols]
            for piece in range(group):
                here = slice(piece * run, (piece + 1) * run)
                r_buf[here, cols] = (x_buf[s, piece, :, cols].astype(F32) + attn[here, :]).astype(BF16)
        for start in range(0, tokens, rows):
            here = pl.ds(start, rows)
            n_buf[here, :] = layer_norm(r_buf[here, :].astype(F32), v_ln2_g[...], v_ln2_c[...]).astype(BF16)
        for block in range(MLP // 256):
            cols = pl.ds(block * 256, 256)
            m_buf[:, cols] = gelu(dot(n_buf[...], v_wup[:, cols]) + v_bup[:, cols]).astype(BF16)
        for block in range(DIM // 256):
            cols = pl.ds(block * 256, 256)
            down = dot(m_buf[...], v_wdown[:, cols])
            h_buf[:, cols] = (r_buf[:, cols].astype(F32) + down + v_bdown[:, cols]).astype(BF16)
        for start in range(0, tokens, rows):
            here = pl.ds(start, rows)
            z_buf[here, :] = layer_norm(h_buf[here, :].astype(F32), v_lnf_g[...], v_lnf_c[...]).astype(BF16)
        h_t[...] = z_buf[...].T
        for part in range(2):
            here = pl.ds(part * DIM, DIM)
            kv_t[here, :] = add_column(dot(v_pwkv[here, :], h_t[...]), col_kv[here, :]).astype(BF16)
        scores = dot(u_diag[...], kv_t[pl.ds(0, DIM), :])
        top = jnp.max(scores, axis=1, keepdims=True)
        weights = jnp.exp2((scores - top) * (LOG2E * HEAD**-0.5))
        total = jnp.sum(weights, axis=1, keepdims=True)
        value = dot_nt(weights.astype(BF16), kv_t[pl.ds(DIM, DIM), :]) / total
        pooled = jnp.sum(jnp.where(diagonal, value, 0.0), axis=0, keepdims=True)
        a_buf[...] = jnp.where(lax.broadcasted_iota(jnp.int32, (8, DIM), 0) == s, pooled, a_buf[...])
        return 0

    lax.fori_loop(0, local, one_image, 0)

    pooled = a_buf[...].astype(BF16)
    o = (dot(pooled, v_pwout[...]) + v_pbout[...]).astype(BF16)
    normed = layer_norm(o.astype(F32), v_plng[...], v_plnc[...]).astype(BF16)
    hidden = gelu(dot(normed, v_pwup[...]) + v_pbup[...]).astype(BF16)
    emb[...] = (o.astype(F32) + dot(hidden, v_pwdown[...]) + v_pbdown[...])[:local, :]

    def share(k):
        return pltpu.make_async_remote_copy(
            src_ref=emb,
            dst_ref=out_ref.at[me],
            send_sem=emb_send.at[k],
            recv_sem=emb_recv.at[k],
            device_id={"cp": me ^ k},
            device_id_type=MESH,
        )

    for k in order:
        share(k).start()
    out_ref[me] = emb[...]
    for s in range(local):
        for k in order:
            send(s, k).wait_send()
    for k in order:
        share(k).wait()


def solution(mesh):
    group = mesh.shape["cp"]

    def device_step(
        images, ln1_scale, ln1_bias, w_qkv, b_qkv, w_out, b_out, ln2_scale, ln2_bias, w_up, b_up, w_down, b_down, lnf_scale, lnf_bias,
        pool_probe, pool_wq, pool_bq, pool_wkv, pool_bkv, pool_wout, pool_bout, pool_ln_scale, pool_ln_bias, pool_w_up, pool_b_up,
        pool_w_down, pool_b_down,
    ):
        count, run, _ = images.shape
        local = count // group
        tokens = group * run

        def row(vector):
            return vector.reshape(1, -1)

        operands = [
            images, row(ln1_scale), row(ln1_bias), w_qkv.transpose(1, 2, 3, 0).reshape(3 * DIM, DIM), b_qkv,
            w_out.reshape(DIM, DIM), row(b_out), row(ln2_scale), row(ln2_bias), w_up, row(b_up), w_down, row(b_down),
            row(lnf_scale), row(lnf_bias), pool_probe, pool_wq.transpose(1, 2, 0).reshape(DIM, DIM), pool_bq,
            pool_wkv.transpose(1, 2, 3, 0).reshape(2 * DIM, DIM), pool_bkv.transpose(1, 0, 2), pool_wout.reshape(DIM, DIM),
            row(pool_bout), row(pool_ln_scale), row(pool_ln_bias), pool_w_up, row(pool_b_up), pool_w_down, row(pool_b_down),
        ]
        held = [pltpu.VMEM(operand.shape, operand.dtype) for operand in operands[1:]]
        scratch = [
            pltpu.VMEM((local, group, run, DIM), BF16),
            *held,
            pltpu.VMEM((DIM, DIM), BF16),
            pltpu.VMEM((3 * DIM, 128), F32),
            pltpu.VMEM((DIM, 128), F32),
            pltpu.VMEM((2 * DIM, 128), F32),
            pltpu.VMEM((1, DIM), F32),
            pltpu.VMEM((16, DIM), BF16),
            pltpu.VMEM((tokens, DIM), BF16),
            pltpu.VMEM((DIM, tokens), BF16),
            pltpu.VMEM((DIM, tokens), BF16),
            pltpu.VMEM((DIM, tokens), BF16),
            pltpu.VMEM((tokens, DIM), BF16),
            pltpu.VMEM((DIM, tokens), BF16),
            pltpu.VMEM((tokens, DIM), BF16),
            pltpu.VMEM((tokens, DIM), BF16),
            pltpu.VMEM((tokens, MLP), BF16),
            pltpu.VMEM((tokens, DIM), BF16),
            pltpu.VMEM((2 * DIM, tokens), BF16),
            pltpu.VMEM((8, DIM), F32),
            pltpu.VMEM((local, DIM), F32),
            pltpu.SemaphoreType.DMA((len(held),)),
            pltpu.SemaphoreType.DMA((local,)),
            pltpu.SemaphoreType.DMA((local, group)),
            pltpu.SemaphoreType.DMA((local, group)),
            pltpu.SemaphoreType.DMA((group,)),
            pltpu.SemaphoreType.DMA((group,)),
        ]
        result = pl.pallas_call(
            functools.partial(kernel, group, local, run),
            out_shape=jax.ShapeDtypeStruct((group, local, DIM), F32),
            in_specs=[pl.BlockSpec(memory_space=pl.ANY)] * len(operands),
            out_specs=pl.BlockSpec(memory_space=pltpu.VMEM),
            scratch_shapes=scratch,
            compiler_params=pltpu.CompilerParams(collective_id=0, has_side_effects=True, vmem_limit_bytes=67_043_328),
        )(*operands)
        return result.reshape(count, DIM)

    in_specs = (P("dp", "cp", None),) + (P(),) * 27
    return jax.shard_map(device_step, mesh=mesh, in_specs=in_specs, out_specs=P("dp", None), check_vma=False)
```

time: 716 us -> 88.4 us (0.12); the launches traced: 707 us -> 87.9 us
  waiting for transfers between devices: 429 us -> 0 us
  matrix products: 146 us -> 0 us
  Pallas kernels: 0 us -> 71.1 us
  local copies, waits for them, and re-layouts: 81.3 us -> 16.8 us
  other arithmetic: 26.9 us -> 0 us
  blocking collectives: 18.6 us -> 0 us
    ppermute x14 -> x0, waiting for transfers between devices: 429 us -> none  [visit_block(): held_kv = lax.ppermute(held_kv, 'cp', send_pairs)]
    dot_general x28 -> x0, matrix products: 146 us -> none  [the longest x8 68 us: block_stats(): jnp.einsum('bhqk,bkhe->bhqe', weights.astype(jnp.bfloat16), value_rows, p...]
    while x70 -> x0, local copies, waits for them, and re-layouts: 80.8 us -> none
    pallas_call x0 -> x1, Pallas kernels: none -> 71.1 us  [device_step(): pl.pallas_call(functools.partial(kernel, group, local, run), out_shape=ja...]
    reduce_sum x16 -> x0, other arithmetic: 22.9 us -> none  [the longest x8 16.6 us: block_stats(): return (row_max, jnp.sum(weights, axis=-1), value_sum)]
    all_gather x1 -> x0, blocking collectives: 18.6 us -> none  [device_step(): gathered = lax.all_gather(local_stats, 'cp')]
    reshape x0 -> x13, local copies, waits for them, and re-layouts: none -> 16.8 us  [the longest x12 15.3 us: row(): return vector.reshape(1, -1)]
  transfers between devices with their start and end apart: 14 -> 0, of which waited for: 14 -> 0; matrix products, arithmetic and copies ran while one was open for 10% -> 0% of each run, Pallas kernels for 0% -> 0%
where the time goes in v1:
time: 88.4 us; the launch traced here: 87.9 us
  Pallas kernels  71.1 us (80%)
  local copies, waits for them, and re-layouts  16.8 us (19%)
    pallas_call x1, Pallas kernels, device_step(): pl.pallas_call(functools.partial(kernel, group, local, run), out_shape=ja...  71.1 us
    reshape x12, local copies, waits for them, and re-layouts, row(): return vector.reshape(1, -1)  15.3 us

profile of v1, /device:TPU:0, one launch (start us, length us, event | category | flops | bytes accessed | tf_op | source)
XLA Modules:
  0.0 87.9 jit_solution(1605228429510993044)
XLA Ops:
  0.0 1.3 %reshape.60.ln1_g = f32[1,768]{1,0:T(1,128)} reshape(f32[768]{0:T(1024)} %param.29) | data formatting | bytes 6144 | tf_op jit(solution)/shard_map/reshape | solution.py:235
  1.3 1.3 %reshape.61.ln1_c = f32[1,768]{1,0:T(1,128)} reshape(f32[768]{0:T(1024)} %param.30) | data formatting | bytes 6144 | tf_op jit(solution)/shard_map/reshape | solution.py:235
  2.6 1.3 %reshape.64.b_out = f32[1,768]{1,0:T(1,128)} reshape(f32[768]{0:T(1024)} %param.34) | data formatting | bytes 6144 | tf_op jit(solution)/shard_map/reshape | solution.py:235
  3.8 1.3 %reshape.65.ln2_g = f32[1,768]{1,0:T(1,128)} reshape(f32[768]{0:T(1024)} %param.35) | data formatting | bytes 6144 | tf_op jit(solution)/shard_map/reshape | solution.py:235
  5.1 1.3 %reshape.66.ln2_c = f32[1,768]{1,0:T(1,128)} reshape(f32[768]{0:T(1024)} %param.36) | data formatting | bytes 6144 | tf_op jit(solution)/shard_map/reshape | solution.py:235
  6.4 1.2 %reshape.68.b_down = f32[1,768]{1,0:T(1,128)} reshape(f32[768]{0:T(1024)} %param.40) | data formatting | bytes 6144 | tf_op jit(solution)/shard_map/reshape | solution.py:235
  7.6 1.3 %reshape.69.lnf_g = f32[1,768]{1,0:T(1,128)} reshape(f32[768]{0:T(1024)} %param.41) | data formatting | bytes 6144 | tf_op jit(solution)/shard_map/reshape | solution.py:235
  8.9 1.3 %reshape.70.lnf_c = f32[1,768]{1,0:T(1,128)} reshape(f32[768]{0:T(1024)} %param.42) | data formatting | bytes 6144 | tf_op jit(solution)/shard_map/reshape | solution.py:235
  10.2 1.3 %reshape.74.p_bout = f32[1,768]{1,0:T(1,128)} reshape(f32[768]{0:T(1024)} %param.49) | data formatting | bytes 6144 | tf_op jit(solution)/shard_map/reshape | solution.py:235
  11.5 1.3 %reshape.75.pln_g = f32[1,768]{1,0:T(1,128)} reshape(f32[768]{0:T(1024)} %param.50) | data formatting | bytes 6144 | tf_op jit(solution)/shard_map/reshape | solution.py:235
  12.7 1.3 %reshape.76.pln_c = f32[1,768]{1,0:T(1,128)} reshape(f32[768]{0:T(1024)} %param.51) | data formatting | bytes 6144 | tf_op jit(solution)/shard_map/reshape | solution.py:235
  14.0 1.3 %reshape.78.p_bdown = f32[1,768]{1,0:T(1,128)} reshape(f32[768]{0:T(1024)} %param.55) | data formatting | bytes 6144 | tf_op jit(solution)/shard_map/reshape | solution.py:235
  15.3 71.1 %shard_map.262 = f32[8,4,768]{2,1,0:T(4,128)} custom-call(bf16[32,32,768]{2,1,0:T(8,128)(2,1)} %images.1, f32[1,768]{1,0:T(1,128)} %reshape.60.ln1_g, f32[1,768]{1,0:T(1,128)} %reshape.61.ln1_c, bf16[2304,768]{1,0:T(8,128)(2,1)} %bitcast.14, f32[3,12,64]{2,1,0:T(8,128)} %b_qkv.1, bf16[768,768]{1,0:T(8,128)(2,1)} %bitcast.16, f32[1,768]{1,0:T(1,128)} %reshape.64.b_out, ...), custom_call_target="tpu_custom_call" | custom-call | tf_op jit(solution)/shard_map/pallas_call | solution.py:274
  86.3 1.6 %reshape.79 = f32[32,768]{1,0:T(8,128)} reshape(f32[8,4,768]{2,1,0:T(4,128)} %shard_map.262) | data formatting | bytes 196608 | tf_op jit(solution)/shard_map/reshape | solution.py:282

commit v2 on v1

--- a/solution.py
+++ b/solution.py
@@ -28,6 +28,10 @@
     return lax.dot_general(left, right, (((1,), (1,)), ((), ())), preferred_element_type=F32)
 
 
+def as_row(ref, cols=slice(None)):
+    return ref[cols][None, :]
+
+
 def gelu(x):
     half = 0.5 * x
     return half + half * jnp.tanh(x * (GELU_C + (GELU_C * 0.044715) * (x * x)))
@@ -68,14 +72,25 @@
     out_ref,
     x_buf, v_ln1_g, v_ln1_c, v_wqkv, v_bqkv, v_wout, v_bout, v_ln2_g, v_ln2_c, v_wup, v_bup, v_wdown, v_bdown, v_lnf_g, v_lnf_c,
     v_probe, v_pwq, v_pbq, v_pwkv, v_pbkv, v_pwout, v_pbout, v_plng, v_plnc, v_pwup, v_pbup, v_pwdown, v_pbdown,
-    wk_t, col_qkv, col_q, col_kv, row_k, u_diag, h_buf, h_t, q_t, v_t, k_buf, c_t, r_buf, n_buf, m_buf, z_buf, kv_t, a_buf, emb,
-    load_sem, own_sem, send_sem, recv_sem, emb_send, emb_recv,
+    wk_t, col_qkv, col_q, col_kv, row_k, u_diag, h_buf, h_t, q_t, v_t, k_buf, c_t, r_buf, n_buf, m_buf, z_buf, kv_t, s_buf, w_buf, t_buf, a_buf, emb,
+    load_sem, own_sem, send_sem, recv_sem, emb_send, emb_recv, relay,
 ):
     tokens = group * run
     me = lax.axis_index("cp")
+    chip = me // 2
+    inner = (chip == 1) | (chip == 2)
+
+    def tell(semaphore, k):
+        pl.semaphore_signal(semaphore, inc=1, device_id={"cp": me ^ k}, device_id_type=MESH)
+
     barrier = pltpu.get_barrier_semaphore()
-    for k in range(1, group):
-        pl.semaphore_signal(barrier, inc=1, device_id={"cp": me ^ k}, device_id_type=MESH)
+    for k in (2, 3, 1):
+        tell(barrier, k)
+
+    @pl.when(inner)
+    def _():
+        tell(barrier, 6)
+        tell(barrier, 7)
 
     pairs = [
         (w_qkv, v_wqkv), (ln1_g, v_ln1_g), (ln1_c, v_ln1_c), (b_qkv, v_bqkv), (w_out, v_wout), (b_out, v_bout),
@@ -102,13 +117,40 @@
             device_id_type=MESH,
         )
 
-    order = sorted(range(1, group), key=lambda k: -k)
-    pl.semaphore_wait(barrier, group - 1)
-    for s in range(local):
-        for k in order:
-            send(s, k).start()
+    far, near = (6, 7, 4, 5), (2, 3, 1)
+    order = far + near
+
+    @pl.when(inner)
+    def _():
+        pl.semaphore_wait(barrier, 5)
+        send(0, 6).start()
+        send(0, 7).start()
+        tell(relay.at[0], 2)
+        tell(relay.at[0], 6)
+
+    @pl.when(jnp.logical_not(inner))
+    def _():
+        pl.semaphore_wait(barrier, 3)
+
+    for k in near:
+        send(0, k).start()
     for copy in loads[4:]:
         copy.start()
+    pl.semaphore_wait(relay.at[0], 1)
+
+    @pl.when(inner)
+    def _():
+        tell(relay.at[1], 2)
+
+    send(0, 4).start()
+    send(0, 5).start()
+
+    @pl.when(jnp.logical_not(inner))
+    def _():
+        pl.semaphore_wait(relay.at[1], 1)
+        send(0, 6).start()
+        send(0, 7).start()
+
     for copy in loads[:4]:
         copy.wait()
 
@@ -130,6 +172,10 @@
 
     rows = 32
     a_buf[...] = jnp.zeros_like(a_buf)
+    for k in far:
+        send(0, k).wait_send()
+    for k in order:
+        send(1, k).start()
 
     def one_image(s, _):
         pltpu.make_async_copy(images.at[0], x_buf.at[s, me], own_sem.at[s]).wait()
@@ -138,66 +184,87 @@
 
         for piece in range(group):
             x = x_buf[s, piece].astype(F32)
-            h_buf[pl.ds(piece * run, run), :] = layer_norm(x, v_ln1_g[...], v_ln1_c[...]).astype(BF16)
+            h_buf[pl.ds(piece * run, run), :] = layer_norm(x, as_row(v_ln1_g), as_row(v_ln1_c)).astype(BF16)
         h_t[...] = h_buf[...].T
+
         q_t[...] = add_column(dot(v_wqkv[pl.ds(0, DIM), :], h_t[...]), col_qkv[pl.ds(0, DIM), :]).astype(BF16)
         v_t[...] = add_column(dot(v_wqkv[pl.ds(2 * DIM, DIM), :], h_t[...]), col_qkv[pl.ds(2 * DIM, DIM), :]).astype(BF16)
         k_buf[...] = (dot(h_buf[...], wk_t[...]) + row_k[...]).astype(BF16)
 
+        pairs = HEADS // 2
         zero = jnp.zeros((HEAD, tokens), BF16)
-        for pair in range(HEADS // 2):
-            k_pair = k_buf[:, pl.ds(pair * 2 * HEAD, 2 * HEAD)]
-            for side in range(2):
-                head = 2 * pair + side
-                q_head = q_t[pl.ds(head * HEAD, HEAD), :]
-                q_pair = jnp.concatenate([q_head, zero] if side == 0 else [zero, q_head], axis=0)
-                scores = dot(k_pair, q_pair)
-                top = jnp.max(scores, axis=0, keepdims=True)
-                weights = jnp.exp2((scores - top) * (LOG2E * HEAD**-0.5))
-                total = jnp.sum(weights, axis=0, keepdims=True)
-                value = dot(v_t[pl.ds(head * HEAD, HEAD), :], weights.astype(BF16))
-                c_t[pl.ds(head * HEAD, HEAD), :] = (value / total).astype(BF16)
+        for step in range(pairs + 2):
+            if step < pairs:
+                k_pair = k_buf[:, pl.ds(step * 2 * HEAD, 2 * HEAD)]
+                low = q_t[pl.ds(2 * step * HEAD, HEAD), :]
+                high = q_t[pl.ds((2 * step + 1) * HEAD, HEAD), :]
+                s_buf[step % 2, :, pl.ds(0, tokens)] = dot(k_pair, jnp.concatenate([low, zero], axis=0))
+                s_buf[step % 2, :, pl.ds(tokens, tokens)] = dot(k_pair, jnp.concatenate([zero, high], axis=0))
+            if 1 <= step <= pairs:
+                slot = (step - 1) % 2
+                for block in range(2 * tokens // 128):
+                    cols = pl.ds(block * 128, 128)
+                    top = jnp.max(s_buf[slot, :, cols], axis=0, keepdims=True)
+                    weights = jnp.exp2((s_buf[slot, :, cols] - top) * (LOG2E * HEAD**-0.5))
+                    t_buf[slot, :, cols] = 1.0 / jnp.sum(weights, axis=0, keepdims=True)
+                    w_buf[slot, :, cols] = weights.astype(BF16)
+            if step >= 2:
+                slot = step % 2
+                for side in range(2):
+                    here = pl.ds((2 * (step - 2) + side) * HEAD, HEAD)
+                    cols = pl.ds(side * tokens, tokens)
+                    c_t[here, :] = (dot(v_t[here, :], w_buf[slot, :, cols]) * t_buf[slot, :, cols]).astype(BF16)
 
         h_buf[...] = c_t[...].T
-        for block in range(DIM // 256):
-            cols = pl.ds(block * 256, 256)
-            attn = dot(h_buf[...], v_wout[:, cols]) + v_bout[:, cols]
-            for piece in range(group):
-                here = slice(piece * run, (piece + 1) * run)
-                r_buf[here, cols] = (x_buf[s, piece, :, cols].astype(F32) + attn[here, :]).astype(BF16)
+
+        attn = dot(h_buf[...], v_wout[...]) + as_row(v_bout)
+        for piece in range(group):
+            here = slice(piece * run, (piece + 1) * run)
+            r_buf[here, :] = (x_buf[s, piece].astype(F32) + attn[here, :]).astype(BF16)
         for start in range(0, tokens, rows):
             here = pl.ds(start, rows)
-            n_buf[here, :] = layer_norm(r_buf[here, :].astype(F32), v_ln2_g[...], v_ln2_c[...]).astype(BF16)
-        for block in range(MLP // 256):
-            cols = pl.ds(block * 256, 256)
-            m_buf[:, cols] = gelu(dot(n_buf[...], v_wup[:, cols]) + v_bup[:, cols]).astype(BF16)
-        for block in range(DIM // 256):
-            cols = pl.ds(block * 256, 256)
-            down = dot(m_buf[...], v_wdown[:, cols])
-            h_buf[:, cols] = (r_buf[:, cols].astype(F32) + down + v_bdown[:, cols]).astype(BF16)
+            n_buf[here, :] = layer_norm(r_buf[here, :].astype(F32), as_row(v_ln2_g), as_row(v_ln2_c)).astype(BF16)
+
+        for block in range(MLP // 512):
+            cols = pl.ds(block * 512, 512)
+            m_buf[:, cols] = gelu(dot(n_buf[...], v_wup[:, cols]) + as_row(v_bup, cols)).astype(BF16)
+
+        down = dot(m_buf[...], v_wdown[...])
+        h_buf[...] = (r_buf[...].astype(F32) + down + as_row(v_bdown)).astype(BF16)
         for start in range(0, tokens, rows):
             here = pl.ds(start, rows)
-            z_buf[here, :] = layer_norm(h_buf[here, :].astype(F32), v_lnf_g[...], v_lnf_c[...]).astype(BF16)
+            z_buf[here, :] = layer_norm(h_buf[here, :].astype(F32), as_row(v_lnf_g), as_row(v_lnf_c)).astype(BF16)
+
         h_t[...] = z_buf[...].T
-        for part in range(2):
-            here = pl.ds(part * DIM, DIM)
+
+        for part in range(4):
+            here = pl.ds(part * (DIM // 2), DIM // 2)
             kv_t[here, :] = add_column(dot(v_pwkv[here, :], h_t[...]), col_kv[here, :]).astype(BF16)
+
+        @pl.when(s < local - 2)
+        def _():
+            for k in order:
+                send(s + 2, k).start()
+
         scores = dot(u_diag[...], kv_t[pl.ds(0, DIM), :])
         top = jnp.max(scores, axis=1, keepdims=True)
         weights = jnp.exp2((scores - top) * (LOG2E * HEAD**-0.5))
         total = jnp.sum(weights, axis=1, keepdims=True)
         value = dot_nt(weights.astype(BF16), kv_t[pl.ds(DIM, DIM), :]) / total
+        head_of_lane = lax.broadcasted_iota(jnp.int32, (16, DIM), 1) // HEAD
+        diagonal = head_of_lane == lax.broadcasted_iota(jnp.int32, (16, DIM), 0)
         pooled = jnp.sum(jnp.where(diagonal, value, 0.0), axis=0, keepdims=True)
         a_buf[...] = jnp.where(lax.broadcasted_iota(jnp.int32, (8, DIM), 0) == s, pooled, a_buf[...])
+
         return 0
 
     lax.fori_loop(0, local, one_image, 0)
 
     pooled = a_buf[...].astype(BF16)
-    o = (dot(pooled, v_pwout[...]) + v_pbout[...]).astype(BF16)
-    normed = layer_norm(o.astype(F32), v_plng[...], v_plnc[...]).astype(BF16)
-    hidden = gelu(dot(normed, v_pwup[...]) + v_pbup[...]).astype(BF16)
-    emb[...] = (o.astype(F32) + dot(hidden, v_pwdown[...]) + v_pbdown[...])[:local, :]
+    o = (dot(pooled, v_pwout[...]) + as_row(v_pbout)).astype(BF16)
+    normed = layer_norm(o.astype(F32), as_row(v_plng), as_row(v_plnc)).astype(BF16)
+    hidden = gelu(dot(normed, v_pwup[...]) + as_row(v_pbup)).astype(BF16)
+    emb[...] = (o.astype(F32) + dot(hidden, v_pwdown[...]) + as_row(v_pbdown))[:local, :]
 
     def share(k):
         return pltpu.make_async_remote_copy(
@@ -212,7 +279,10 @@
     for k in order:
         share(k).start()
     out_ref[me] = emb[...]
-    for s in range(local):
+    for k in order:
+        if k not in far:
+            send(0, k).wait_send()
+    for s in range(1, local):
         for k in order:
             send(s, k).wait_send()
     for k in order:
@@ -231,15 +301,12 @@
         local = count // group
         tokens = group * run
 
-        def row(vector):
-            return vector.reshape(1, -1)
-
         operands = [
-            images, row(ln1_scale), row(ln1_bias), w_qkv.transpose(1, 2, 3, 0).reshape(3 * DIM, DIM), b_qkv,
-            w_out.reshape(DIM, DIM), row(b_out), row(ln2_scale), row(ln2_bias), w_up, row(b_up), w_down, row(b_down),
-            row(lnf_scale), row(lnf_bias), pool_probe, pool_wq.transpose(1, 2, 0).reshape(DIM, DIM), pool_bq,
+            images, ln1_scale, ln1_bias, w_qkv.transpose(1, 2, 3, 0).reshape(3 * DIM, DIM), b_qkv,
+            w_out.reshape(DIM, DIM), b_out, ln2_scale, ln2_bias, w_up, b_up, w_down, b_down,
+            lnf_scale, lnf_bias, pool_probe, pool_wq.transpose(1, 2, 0).reshape(DIM, DIM), pool_bq,
             pool_wkv.transpose(1, 2, 3, 0).reshape(2 * DIM, DIM), pool_bkv.transpose(1, 0, 2), pool_wout.reshape(DIM, DIM),
-            row(pool_bout), row(pool_ln_scale), row(pool_ln_bias), pool_w_up, row(pool_b_up), pool_w_down, row(pool_b_down),
+            pool_bout, pool_ln_scale, pool_ln_bias, pool_w_up, pool_b_up, pool_w_down, pool_b_down,
         ]
         held = [pltpu.VMEM(operand.shape, operand.dtype) for operand in operands[1:]]
         scratch = [
@@ -262,6 +329,9 @@
             pltpu.VMEM((tokens, MLP), BF16),
             pltpu.VMEM((tokens, DIM), BF16),
             pltpu.VMEM((2 * DIM, tokens), BF16),
+            pltpu.VMEM((2, tokens, 2 * tokens), F32),
+            pltpu.VMEM((2, tokens, 2 * tokens), BF16),
+            pltpu.VMEM((2, 1, 2 * tokens), F32),
             pltpu.VMEM((8, DIM), F32),
             pltpu.VMEM((local, DIM), F32),
             pltpu.SemaphoreType.DMA((len(held),)),
@@ -270,6 +340,7 @@
             pltpu.SemaphoreType.DMA((local, group)),
             pltpu.SemaphoreType.DMA((group,)),
             pltpu.SemaphoreType.DMA((group,)),
+            pltpu.SemaphoreType.REGULAR((2,)),
         ]
         result = pl.pallas_call(
             functools.partial(kernel, group, local, run),

time: 88.4 us -> 56.4 us (0.64)
  Pallas kernels: 71.1 us -> 54.7 us
  local copies, waits for them, and re-layouts: 16.8 us -> 1.57 us
    pallas_call x1, Pallas kernels: 71.1 us -> 54.7 us  [device_step(): pl.pallas_call(functools.partial(kernel, group, local, run), out_shape=ja...]
    reshape x12 -> x0, local copies, waits for them, and re-layouts: 15.3 us -> none  [row(): return vector.reshape(1, -1)]
where the time goes in v2:
time: 56.4 us; the launch traced here: 56.3 us
  Pallas kernels  54.7 us (97%)
  local copies, waits for them, and re-layouts  1.57 us (3%)
    pallas_call x1, Pallas kernels, device_step(): pl.pallas_call(functools.partial(kernel, group, local, run), out_shape=ja...  54.7 us
    reshape x1, local copies, waits for them, and re-layouts, device_step(): return result.reshape(count, DIM)  1.57 us

profile of v2, /device:TPU:0, one launch (start us, length us, event | category | flops | bytes accessed | tf_op | source)
XLA Modules:
  0.0 56.3 jit_solution(6632066906291779480)
XLA Ops:
  0.0 54.7 %shard_map.262 = f32[8,4,768]{2,1,0:T(4,128)} custom-call(bf16[32,32,768]{2,1,0:T(8,128)(2,1)} %images.1, f32[768]{0:T(1024)} %ln1_g.1, f32[768]{0:T(1024)} %ln1_c.1, bf16[2304,768]{1,0:T(8,128)(2,1)} %bitcast.12, f32[3,12,64]{2,1,0:T(8,128)} %b_qkv.1, bf16[768,768]{1,0:T(8,128)(2,1)} %bitcast.14, f32[768]{0:T(1024)} %b_out.1, f32[768]{0:T(1024)} %ln2_g.1, ...), custom_call_target="tpu_custom_call" | custom-call | tf_op jit(solution)/shard_map/pallas_call | solution.py:345
  54.7 1.6 %reshape.23 = f32[32,768]{1,0:T(8,128)} reshape(f32[8,4,768]{2,1,0:T(4,128)} %shard_map.262) | data formatting | bytes 196608 | tf_op jit(solution)/shard_map/reshape | solution.py:353

commit v3 on v2

--- a/solution.py
+++ b/solution.py
@@ -164,6 +164,11 @@
     column_bias(v_pbq[...], col_q, 0)
     column_bias(v_pbkv[:, 0, :], col_kv, 0)
     column_bias(v_pbkv[:, 1, :], col_kv, DIM)
+    @pl.when(jnp.logical_not(inner))
+    def _():
+        for k in order:
+            send(1, k).start()
+
     probe_rows = jnp.broadcast_to(v_probe[...].astype(F32), (16, DIM)).astype(BF16)
     probe_q = dot_nt(probe_rows, v_pwq[...]) + row_bias(col_q, 0)
     head_of_lane = lax.broadcasted_iota(jnp.int32, (16, DIM), 1) // HEAD
@@ -172,19 +177,26 @@
 
     rows = 32
     a_buf[...] = jnp.zeros_like(a_buf)
-    for k in far:
-        send(0, k).wait_send()
-    for k in order:
-        send(1, k).start()
+
+    @pl.when(inner)
+    def _():
+        for k in far:
+            send(0, k).wait_send()
+        for k in order:
+            send(1, k).start()
+
 
     def one_image(s, _):
         pltpu.make_async_copy(images.at[0], x_buf.at[s, me], own_sem.at[s]).wait()
-        for k in order:
-            send(s, k).wait_recv()
-
-        for piece in range(group):
-            x = x_buf[s, piece].astype(F32)
-            h_buf[pl.ds(piece * run, run), :] = layer_norm(x, as_row(v_ln1_g), as_row(v_ln1_c)).astype(BF16)
+        for ks in (near + (0,), far):
+            for k in ks:
+                if k:
+                    send(s, k).wait_recv()
+            for k in ks:
+                here = pl.ds(pl.multiple_of((me ^ k) * run, run), run)
+                x = x_buf[s, me ^ k].astype(F32)
+                h_buf[here, :] = layer_norm(x, as_row(v_ln1_g), as_row(v_ln1_c)).astype(BF16)
+
         h_t[...] = h_buf[...].T
 
         q_t[...] = add_column(dot(v_wqkv[pl.ds(0, DIM), :], h_t[...]), col_qkv[pl.ds(0, DIM), :]).astype(BF16)
@@ -217,36 +229,37 @@
 
         h_buf[...] = c_t[...].T
 
-        attn = dot(h_buf[...], v_wout[...]) + as_row(v_bout)
-        for piece in range(group):
-            here = slice(piece * run, (piece + 1) * run)
-            r_buf[here, :] = (x_buf[s, piece].astype(F32) + attn[here, :]).astype(BF16)
-        for start in range(0, tokens, rows):
-            here = pl.ds(start, rows)
-            n_buf[here, :] = layer_norm(r_buf[here, :].astype(F32), as_row(v_ln2_g), as_row(v_ln2_c)).astype(BF16)
-
-        for block in range(MLP // 512):
-            cols = pl.ds(block * 512, 512)
-            m_buf[:, cols] = gelu(dot(n_buf[...], v_wup[:, cols]) + as_row(v_bup, cols)).astype(BF16)
-
-        down = dot(m_buf[...], v_wdown[...])
-        h_buf[...] = (r_buf[...].astype(F32) + down + as_row(v_bdown)).astype(BF16)
-        for start in range(0, tokens, rows):
-            here = pl.ds(start, rows)
-            z_buf[here, :] = layer_norm(h_buf[here, :].astype(F32), as_row(v_lnf_g), as_row(v_lnf_c)).astype(BF16)
-
+        half_rows = tokens // 2
+        for half in range(2):
+            here = pl.ds(half * half_rows, half_rows)
+            attn = dot(h_buf[here, :], v_wout[...]) + as_row(v_bout)
+            for part in range(group // 2):
+                piece = half * (group // 2) + part
+                r_buf[pl.ds(piece * run, run), :] = (x_buf[s, piece].astype(F32) + attn[part * run : (part + 1) * run, :]).astype(BF16)
+            for start in range(0, half_rows, rows):
+                some = pl.ds(half * half_rows + start, rows)
+                n_buf[some, :] = layer_norm(r_buf[some, :].astype(F32), as_row(v_ln2_g), as_row(v_ln2_c)).astype(BF16)
+        for half in range(2):
+            here = pl.ds(half * half_rows, half_rows)
+            for block in range(MLP // 512):
+                cols = pl.ds(block * 512, 512)
+                m_buf[here, cols] = gelu(dot(n_buf[here, :], v_wup[:, cols]) + as_row(v_bup, cols)).astype(BF16)
+        for half in range(2):
+            here = pl.ds(half * half_rows, half_rows)
+            down = dot(m_buf[here, :], v_wdown[...])
+            h_buf[here, :] = (r_buf[here, :].astype(F32) + down + as_row(v_bdown)).astype(BF16)
+            for start in range(0, half_rows, rows):
+                some = pl.ds(half * half_rows + start, rows)
+                z_buf[some, :] = layer_norm(h_buf[some, :].astype(F32), as_row(v_lnf_g), as_row(v_lnf_c)).astype(BF16)
         h_t[...] = z_buf[...].T
 
-        for part in range(4):
+        for part in range(2):
             here = pl.ds(part * (DIM // 2), DIM // 2)
             kv_t[here, :] = add_column(dot(v_pwkv[here, :], h_t[...]), col_kv[here, :]).astype(BF16)
-
-        @pl.when(s < local - 2)
-        def _():
-            for k in order:
-                send(s + 2, k).start()
-
         scores = dot(u_diag[...], kv_t[pl.ds(0, DIM), :])
+        for part in range(2, 4):
+            here = pl.ds(part * (DIM // 2), DIM // 2)
+            kv_t[here, :] = add_column(dot(v_pwkv[here, :], h_t[...]), col_kv[here, :]).astype(BF16)
         top = jnp.max(scores, axis=1, keepdims=True)
         weights = jnp.exp2((scores - top) * (LOG2E * HEAD**-0.5))
         total = jnp.sum(weights, axis=1, keepdims=True)
@@ -256,6 +269,11 @@
         pooled = jnp.sum(jnp.where(diagonal, value, 0.0), axis=0, keepdims=True)
         a_buf[...] = jnp.where(lax.broadcasted_iota(jnp.int32, (8, DIM), 0) == s, pooled, a_buf[...])
 
+        @pl.when(s < local - 2)
+        def _():
+            for k in order:
+                send(s + 2, k).start()
+
         return 0
 
     lax.fori_loop(0, local, one_image, 0)
@@ -269,7 +287,7 @@
     def share(k):
         return pltpu.make_async_remote_copy(
             src_ref=emb,
-            dst_ref=out_ref.at[me],
+            dst_ref=out_ref.at[pl.ds(pl.multiple_of(me * local, local), local)],
             send_sem=emb_send.at[k],
             recv_sem=emb_recv.at[k],
             device_id={"cp": me ^ k},
@@ -278,10 +296,17 @@
 
     for k in order:
         share(k).start()
-    out_ref[me] = emb[...]
-    for k in order:
-        if k not in far:
+    mine = pltpu.make_async_copy(emb, out_ref.at[pl.ds(pl.multiple_of(me * local, local), local)], emb_send.at[0])
+    mine.start()
+    mine.wait()
+    for k in near:
+        send(0, k).wait_send()
+
+    @pl.when(jnp.logical_not(inner))
+    def _():
+        for k in far:
             send(0, k).wait_send()
+
     for s in range(1, local):
         for k in order:
             send(s, k).wait_send()
@@ -344,13 +369,13 @@
         ]
         result = pl.pallas_call(
             functools.partial(kernel, group, local, run),
-            out_shape=jax.ShapeDtypeStruct((group, local, DIM), F32),
+            out_shape=jax.ShapeDtypeStruct((count, DIM), F32),
             in_specs=[pl.BlockSpec(memory_space=pl.ANY)] * len(operands),
-            out_specs=pl.BlockSpec(memory_space=pltpu.VMEM),
+            out_specs=pl.BlockSpec(memory_space=pl.ANY),
             scratch_shapes=scratch,
             compiler_params=pltpu.CompilerParams(collective_id=0, has_side_effects=True, vmem_limit_bytes=67_043_328),
         )(*operands)
-        return result.reshape(count, DIM)
+        return result
 
     in_specs = (P("dp", "cp", None),) + (P(),) * 27
     return jax.shard_map(device_step, mesh=mesh, in_specs=in_specs, out_specs=P("dp", None), check_vma=False)

time: 56.4 us -> 54.5 us (0.966)
  Pallas kernels: 54.7 us -> 52.8 us
    pallas_call x1, Pallas kernels: 54.7 us -> 52.8 us  [device_step(): pl.pallas_call(functools.partial(kernel, group, local, run), out_shape=ja...]
    reshape x1 -> x0, local copies, waits for them, and re-layouts: 1.57 us -> none  [device_step(): return result.reshape(count, DIM)]
    unnamed x0 -> x1, local copies, waits for them, and re-layouts: none -> 1.54 us
where the time goes in v3:
time: 54.5 us; the launch traced here: 54.4 us
  Pallas kernels  52.8 us (97%)
  local copies, waits for them, and re-layouts  1.54 us (3%)
    pallas_call x1, Pallas kernels, device_step(): pl.pallas_call(functools.partial(kernel, group, local, run), out_shape=ja...  52.8 us
    unnamed x1, local copies, waits for them, and re-layouts  1.54 us

profile of v3, /device:TPU:0, one launch (start us, length us, event | category | flops | bytes accessed | tf_op | source)
XLA Modules:
  0.0 54.4 jit_solution(17781716131806477626)
XLA Ops:
  0.0 52.8 %shard_map.262 = f32[32,768]{1,0:T(8,128)} custom-call(bf16[32,32,768]{2,1,0:T(8,128)(2,1)} %images.1, f32[768]{0:T(1024)} %ln1_g.1, f32[768]{0:T(1024)} %ln1_c.1, bf16[2304,768]{1,0:T(8,128)(2,1)} %bitcast.12, f32[3,12,64]{2,1,0:T(8,128)} %b_qkv.1, bf16[768,768]{1,0:T(8,128)(2,1)} %bitcast.14, f32[768]{0:T(1024)} %b_out.1, f32[768]{0:T(1024)} %ln2_g.1, ...), custom_call_target="tpu_custom_call" | custom-call | tf_op jit(solution)/shard_map/pallas_call | solution.py:370
  52.9 1.5 %copy.30 = f32[32,768]{1,0:T(8,128)} copy(f32[32,768]{1,0:T(8,128)} %shard_map.262) | data formatting | bytes 196608
